TPU v7x, 256 devices: a whole 4x4x8 slice. The times are simulated.
256 devices in a mesh: pipe: 8 (over x, z_lo), tensor: 4 (over y), expert: 8 (over z_hi, core).
Axes of the slice: x: 4, y: 4, z: 8 (z_hi: 4, z_lo: 2; z = z_hi * 2 + z_lo), core: 2. Of those that a mesh axis runs over, the one named last changes fastest.
Arguments:
- tokens: bfloat16 [2, 512, 4096], P(None, 'expert'), may hold values from -6 to 6
- gains: float32 [8, 4096], P('pipe'), may hold values from 0.1 to 1.9
- route_ids: int32 [8, 2, 512, 2], P('pipe', None, 'expert'), may hold values from 0 to 7, all different within a row
- route_weights: float32 [8, 2, 512, 2], P('pipe', None, 'expert'), may hold values from 0.2 to 1
- picks: int32 [8, 2, 8, 64], P('pipe', None, 'expert'), may hold values from 0 to 63, each once within a row
- w_gate: bfloat16 [8, 8, 4096, 1536], P('pipe', 'expert', None, 'tensor'), may hold values from -0.09375 to 0.09375
- w_up: bfloat16 [8, 8, 4096, 1536], P('pipe', 'expert', None, 'tensor'), may hold values from -0.09375 to 0.09375
- w_down: bfloat16 [8, 8, 1536, 4096], P('pipe', 'expert', 'tensor'), may hold values from -0.15625 to 0.15625
Outputs:
- streams: bfloat16 [8, 2, 512, 4096], P('pipe', None, 'expert', 'tensor')
Inputs may be any that keep to these rules, and one draw needn't show every extreme that they name: `route_ids`: each token names 2 different experts; every expert is named by some token. `picks`: for every layer, micro-batch and block of 64 tokens, a permutation of 0 to 63.
All inputs are finite; a program needn't handle non-finite values.
Results may differ from a plain program's by a relative error of at most 0.025.
Values may be sent and summed in bfloat16 or wider, within the bound.
A program may use at most 64 MiB of HBM per device.

v0:
```python
import jax
import jax.numpy as jnp
from jax import lax
from jax.sharding import PartitionSpec as P

epsilon = 1e-06


def from_everyone(value, axis):
    copies = jnp.broadcast_to(value, (lax.axis_size(axis), *value.shape))
    return lax.all_to_all(copies, axis, split_axis=0, concat_axis=0, tiled=True)


def joined_along(pieces, dim):
    pieces = jnp.moveaxis(pieces, 0, dim)
    shape = pieces.shape
    return pieces.reshape(*shape[:dim], shape[dim] * shape[dim + 1], *shape[dim + 2 :])


def gather_directly(value, axis, dim):
    pieces = from_everyone(value, axis)
    return joined_along(pieces, dim)


def cut_along(value, dim, count):
    before, after = (value.shape[:dim], value.shape[dim + 1 :])
    return jnp.moveaxis(value.reshape(*before, count, -1, *after), dim, 0)


def sum_at_owner(value, axis, dim):
    pieces = cut_along(value, dim, lax.axis_size(axis))
    arrived = lax.all_to_all(pieces, axis, split_axis=0, concat_axis=0, tiled=True)
    return arrived.astype(jnp.float32).sum(axis=0)


def passed_along(block, axis, distance):
    devices = range(lax.axis_size(axis))
    route = [(i - distance, i) for i in devices if i - distance in devices]
    return lax.ppermute(block, axis, route)


def local(tokens, gains, route_ids, route_weights, picks, w_gate, w_up, w_down):
    micro_count = tokens.shape[0]
    local_tokens = tokens.shape[1]
    model_width = tokens.shape[2]
    route_count = route_ids.shape[3]
    tensor_ranks = lax.axis_size("tensor")
    groups = lax.axis_size("expert")
    sections = lax.axis_size("pipe")
    quarter = local_tokens // tensor_ranks
    capacity = 4 * quarter * route_count // (3 * groups)
    slice_width = model_width // tensor_ranks
    my_section = lax.axis_index("pipe")
    my_rank = lax.axis_index("tensor")
    gain_row = gains[0]
    gate_matrix = w_gate[0, 0]
    up_matrix = w_up[0, 0]
    down_matrix = w_down[0, 0]

    def expert_work(arrived):
        gathered = gather_directly(arrived, "tensor", 0)
        row_count = gathered.shape[0] * gathered.shape[1]
        row_block = gathered.reshape(row_count, model_width)
        gate_val = jnp.dot(row_block, gate_matrix, preferred_element_type=jnp.float32)
        up_val = jnp.dot(row_block, up_matrix, preferred_element_type=jnp.float32)
        hidden = (jax.nn.silu(gate_val) * up_val).astype(jnp.bfloat16)
        partial_sum = jnp.dot(hidden, down_matrix, preferred_element_type=jnp.float32)
        summed = sum_at_owner(partial_sum.reshape(gathered.shape).astype(jnp.bfloat16), "tensor", 0)
        return summed.astype(jnp.bfloat16)

    def expert_layer(quarter_rows, chosen, micro_index):
        section_ids = route_ids[0, micro_index][chosen]
        section_weights = route_weights[0, micro_index][chosen]
        stream_f = quarter_rows.astype(jnp.float32)
        inv_rms = lax.rsqrt(jnp.mean(stream_f * stream_f, axis=1, keepdims=True) + epsilon)
        normed = (stream_f * inv_rms * gain_row[None, :]).astype(jnp.bfloat16)
        flat_ids = section_ids.reshape(-1)
        onehot = (flat_ids[:, None] == jnp.arange(groups, dtype=jnp.int32)[None, :]).astype(
            jnp.int32
        )
        earlier = jnp.cumsum(onehot, axis=0) - onehot
        slot_index = jnp.sum(earlier * onehot, axis=1)
        kept_mask = slot_index < capacity
        target = jnp.where(kept_mask, flat_ids * capacity + slot_index, groups * capacity)
        placing = (
            jnp.arange(groups * capacity, dtype=jnp.int32)[:, None] == target[None, :]
        ).astype(jnp.bfloat16)
        routed = jnp.repeat(normed, route_count, axis=0)
        outgoing = jnp.dot(placing, routed, preferred_element_type=jnp.float32).astype(jnp.bfloat16)
        outgoing = outgoing.reshape(groups, capacity, model_width)
        returned = expert_work(
            lax.all_to_all(outgoing, "expert", split_axis=0, concat_axis=0, tiled=True)
        )
        homeward = lax.all_to_all(returned, "expert", split_axis=0, concat_axis=0, tiled=True)
        flat_back = jnp.concatenate(
            [
                homeward.reshape(groups * capacity, model_width),
                jnp.zeros((1, model_width), jnp.bfloat16),
            ],
            axis=0,
        )
        picked = flat_back[target].astype(jnp.float32).reshape(quarter, route_count, model_width)
        kept_grid = kept_mask.reshape(quarter, route_count)
        weighted = picked * (section_weights * kept_grid)[..., None]
        update = jnp.sum(weighted, axis=1)
        return (stream_f + update).astype(jnp.bfloat16)

    def run_section(stream, micro_index):
        order_all = picks[0, micro_index, 0]
        chosen = lax.dynamic_slice_in_dim(order_all, my_rank * quarter, quarter)
        permuted = stream[order_all]
        quarter_rows = lax.all_to_all(permuted, "tensor", split_axis=0, concat_axis=1, tiled=True)
        fresh_rows = expert_layer(quarter_rows, chosen, micro_index)
        spread = lax.all_to_all(fresh_rows, "tensor", split_axis=1, concat_axis=0, tiled=True)
        return jnp.zeros_like(stream).at[order_all].set(spread)

    def first_input(micro_index):
        whole = tokens[micro_index]
        return lax.dynamic_slice_in_dim(whole, my_rank * slice_width, slice_width, 1)

    def send_on(fresh):
        return passed_along(fresh, "pipe", 1)

    def section_tick(carry, tick_index):
        arrived, collected = carry
        micro_index = tick_index - my_section
        active = (micro_index >= 0) & (micro_index < micro_count)
        clipped = jnp.clip(micro_index, 0, micro_count - 1)
        stream = jnp.where(my_section == 0, first_input(clipped), arrived)
        computed = run_section(stream, clipped)
        fresh = jnp.where(active, computed, stream)
        written = collected.at[clipped].set(fresh)
        collected = jnp.where(active, written, collected)
        return ((send_on(fresh), collected), None)

    empty_state = jnp.zeros((local_tokens, slice_width), jnp.bfloat16)
    collected = jnp.zeros((micro_count, local_tokens, slice_width), jnp.bfloat16)
    ticks = jnp.arange(micro_count + sections - 1, dtype=jnp.int32)
    (final_state, collected), unused = lax.scan(section_tick, (empty_state, collected), ticks)
    return collected[None]


def solution(mesh):
    return jax.shard_map(
        local,
        mesh=mesh,
        in_specs=(
            P(None, "expert", None),
            P("pipe", None),
            P("pipe", None, "expert", None),
            P("pipe", None, "expert", None),
            P("pipe", None, "expert", None),
            P("pipe", "expert", None, "tensor"),
            P("pipe", "expert", None, "tensor"),
            P("pipe", "expert", "tensor", None),
        ),
        out_specs=P("pipe", None, "expert", "tensor"),
        check_vma=False,
    )
```

profile of v0, /device:TPU:32, one launch (start us, length us, event | category | flops | bytes accessed | tf_op | source)
XLA Modules:
  0.0 1171.1 jit_solution(10860606724604831986)
XLA Ops:
  1.3 1169.9 %while.16 = (s32[]{:T(128)}, bf16[64,1024]{1,0:T(8,128)(2,1)S(1)}, bf16[2,64,1024]{2,1,0:T(8,128)(2,1)}, s32[9]{0:T(128)}, s32[]{:T(128)}, /*index=5*/s32[1,2,1,...) while((s32[]{:T(128)}, bf16[64,1024]{1,0:T(8,128)(2,1)S(1)}, ...), condition=%wide.region_8.9_spmd, body=%wide.region_0.8_spmd.sunk | while | flops 1523243264 | bytes 51076840 | solution.py:139
  17.6 23.8 %all_to_all.92 = bf16[8,5,4096]{2,1,0:T(8,128)(2,1)S(1)} all-to-all(bf16[8,5,4096]{2,1,0:T(8,128)(2,1)S(1)} %reshape.340), channel_id=1, replica_groups=mesh['pipe'=8,'tensor'=4,'expert'=8] {'expert'}, dimensions={0} | all-to-all | bytes 655360 | tf_op jit(solution)/shard_map/while/body/eval_jaxpr/all_to_all | solution.py:92
  41.7 20.4 %all_to_all.93 = bf16[4,8,5,4096]{3,1,2,0:T(8,128)(2,1)S(1)} all-to-all(bf16[4,8,5,4096]{3,1,2,0:T(8,128)(2,1)S(1)} %broadcast_in_dim.48), channel_id=1, replica_groups=mesh['pipe'=8,'tensor'=4,'expert'=8] {'tensor'}, dimensions={0} | all-to-all | bytes 2621440 | tf_op jit(solution)/shard_map/while/body/eval_jaxpr/all_to_all | solution.py:11
  99.6 17.0 %all-to-all-done.4 = bf16[8,5,4096]{2,1,0:T(8,128)(2,1)S(1)} async-done(((bf16[8,5,4096]{2,1,0:T(8,128)(2,1)}), bf16[8,5,4096]{2,1,0:T(8,128)(2,1)S(1)}, u32[]{:S(2)}, u32[]{:S(2)}) %all-to-all-start.4) | async-done | bytes 327712 | tf_op jit(solution)/shard_map/while/body/eval_jaxpr/all_to_all | solution.py:94
  152.3 19.0 %all_to_all.92 = bf16[8,5,4096]{2,1,0:T(8,128)(2,1)S(1)} all-to-all(bf16[8,5,4096]{2,1,0:T(8,128)(2,1)S(1)} %reshape.340), channel_id=1, replica_groups=mesh['pipe'=8,'tensor'=4,'expert'=8] {'expert'}, dimensions={0} | all-to-all | bytes 655360 | tf_op jit(solution)/shard_map/while/body/eval_jaxpr/all_to_all | solution.py:92
  171.6 20.7 %all_to_all.93 = bf16[4,8,5,4096]{3,1,2,0:T(8,128)(2,1)S(1)} all-to-all(bf16[4,8,5,4096]{3,1,2,0:T(8,128)(2,1)S(1)} %broadcast_in_dim.48), channel_id=1, replica_groups=mesh['pipe'=8,'tensor'=4,'expert'=8] {'tensor'}, dimensions={0} | all-to-all | bytes 2621440 | tf_op jit(solution)/shard_map/while/body/eval_jaxpr/all_to_all | solution.py:11
  280.4 19.1 %all_to_all.92 = bf16[8,5,4096]{2,1,0:T(8,128)(2,1)S(1)} all-to-all(bf16[8,5,4096]{2,1,0:T(8,128)(2,1)S(1)} %reshape.340), channel_id=1, replica_groups=mesh['pipe'=8,'tensor'=4,'expert'=8] {'expert'}, dimensions={0} | all-to-all | bytes 655360 | tf_op jit(solution)/shard_map/while/body/eval_jaxpr/all_to_all | solution.py:92
  299.9 20.7 %all_to_all.93 = bf16[4,8,5,4096]{3,1,2,0:T(8,128)(2,1)S(1)} all-to-all(bf16[4,8,5,4096]{3,1,2,0:T(8,128)(2,1)S(1)} %broadcast_in_dim.48), channel_id=1, replica_groups=mesh['pipe'=8,'tensor'=4,'expert'=8] {'tensor'}, dimensions={0} | all-to-all | bytes 2621440 | tf_op jit(solution)/shard_map/while/body/eval_jaxpr/all_to_all | solution.py:11
  335.4 17.0 %all-to-all-done.3 = bf16[4,8,5,4096]{3,1,2,0:T(8,128)(2,1)S(1)} async-done(((bf16[4,8,5,4096]{3,1,2,0:T(8,128)(2,1)}), bf16[4,8,5,4096]{3,1,2,0:T(8,128)(2,1)S(1)}, u32[]{:S(2)}, u32[]{:S(2)}) %all-to-all-start.3) | async-done | bytes 1310752 | tf_op jit(solution)/shard_map/while/body/eval_jaxpr/all_to_all | solution.py:32
  408.8 20.4 %all_to_all.92 = bf16[8,5,4096]{2,1,0:T(8,128)(2,1)S(1)} all-to-all(bf16[8,5,4096]{2,1,0:T(8,128)(2,1)S(1)} %reshape.340), channel_id=1, replica_groups=mesh['pipe'=8,'tensor'=4,'expert'=8] {'expert'}, dimensions={0} | all-to-all | bytes 655360 | tf_op jit(solution)/shard_map/while/body/eval_jaxpr/all_to_all | solution.py:92
  429.6 20.7 %all_to_all.93 = bf16[4,8,5,4096]{3,1,2,0:T(8,128)(2,1)S(1)} all-to-all(bf16[4,8,5,4096]{3,1,2,0:T(8,128)(2,1)S(1)} %broadcast_in_dim.48), channel_id=1, replica_groups=mesh['pipe'=8,'tensor'=4,'expert'=8] {'tensor'}, dimensions={0} | all-to-all | bytes 2621440 | tf_op jit(solution)/shard_map/while/body/eval_jaxpr/all_to_all | solution.py:11
  465.1 17.0 %all-to-all-done.3 = bf16[4,8,5,4096]{3,1,2,0:T(8,128)(2,1)S(1)} async-done(((bf16[4,8,5,4096]{3,1,2,0:T(8,128)(2,1)}), bf16[4,8,5,4096]{3,1,2,0:T(8,128)(2,1)S(1)}, u32[]{:S(2)}, u32[]{:S(2)}) %all-to-all-start.3) | async-done | bytes 1310752 | tf_op jit(solution)/shard_map/while/body/eval_jaxpr/all_to_all | solution.py:32
  537.6 21.3 %all_to_all.92 = bf16[8,5,4096]{2,1,0:T(8,128)(2,1)S(1)} all-to-all(bf16[8,5,4096]{2,1,0:T(8,128)(2,1)S(1)} %reshape.340), channel_id=1, replica_groups=mesh['pipe'=8,'tensor'=4,'expert'=8] {'expert'}, dimensions={0} | all-to-all | bytes 655360 | tf_op jit(solution)/shard_map/while/body/eval_jaxpr/all_to_all | solution.py:92
  559.3 20.7 %all_to_all.93 = bf16[4,8,5,4096]{3,1,2,0:T(8,128)(2,1)S(1)} all-to-all(bf16[4,8,5,4096]{3,1,2,0:T(8,128)(2,1)S(1)} %broadcast_in_dim.48), channel_id=1, replica_groups=mesh['pipe'=8,'tensor'=4,'expert'=8] {'tensor'}, dimensions={0} | all-to-all | bytes 2621440 | tf_op jit(solution)/shard_map/while/body/eval_jaxpr/all_to_all | solution.py:11
  667.4 21.3 %all_to_all.92 = bf16[8,5,4096]{2,1,0:T(8,128)(2,1)S(1)} all-to-all(bf16[8,5,4096]{2,1,0:T(8,128)(2,1)S(1)} %reshape.340), channel_id=1, replica_groups=mesh['pipe'=8,'tensor'=4,'expert'=8] {'expert'}, dimensions={0} | all-to-all | bytes 655360 | tf_op jit(solution)/shard_map/while/body/eval_jaxpr/all_to_all | solution.py:92
  689.1 20.7 %all_to_all.93 = bf16[4,8,5,4096]{3,1,2,0:T(8,128)(2,1)S(1)} all-to-all(bf16[4,8,5,4096]{3,1,2,0:T(8,128)(2,1)S(1)} %broadcast_in_dim.48), channel_id=1, replica_groups=mesh['pipe'=8,'tensor'=4,'expert'=8] {'tensor'}, dimensions={0} | all-to-all | bytes 2621440 | tf_op jit(solution)/shard_map/while/body/eval_jaxpr/all_to_all | solution.py:11
  797.1 21.3 %all_to_all.92 = bf16[8,5,4096]{2,1,0:T(8,128)(2,1)S(1)} all-to-all(bf16[8,5,4096]{2,1,0:T(8,128)(2,1)S(1)} %reshape.340), channel_id=1, replica_groups=mesh['pipe'=8,'tensor'=4,'expert'=8] {'expert'}, dimensions={0} | all-to-all | bytes 655360 | tf_op jit(solution)/shard_map/while/body/eval_jaxpr/all_to_all | solution.py:92
  818.8 20.7 %all_to_all.93 = bf16[4,8,5,4096]{3,1,2,0:T(8,128)(2,1)S(1)} all-to-all(bf16[4,8,5,4096]{3,1,2,0:T(8,128)(2,1)S(1)} %broadcast_in_dim.48), channel_id=1, replica_groups=mesh['pipe'=8,'tensor'=4,'expert'=8] {'tensor'}, dimensions={0} | all-to-all | bytes 2621440 | tf_op jit(solution)/shard_map/while/body/eval_jaxpr/all_to_all | solution.py:11
  854.3 17.0 %all-to-all-done.3 = bf16[4,8,5,4096]{3,1,2,0:T(8,128)(2,1)S(1)} async-done(((bf16[4,8,5,4096]{3,1,2,0:T(8,128)(2,1)}), bf16[4,8,5,4096]{3,1,2,0:T(8,128)(2,1)S(1)}, u32[]{:S(2)}, u32[]{:S(2)}) %all-to-all-start.3) | async-done | bytes 1310752 | tf_op jit(solution)/shard_map/while/body/eval_jaxpr/all_to_all | solution.py:32
  926.8 21.3 %all_to_all.92 = bf16[8,5,4096]{2,1,0:T(8,128)(2,1)S(1)} all-to-all(bf16[8,5,4096]{2,1,0:T(8,128)(2,1)S(1)} %reshape.340), channel_id=1, replica_groups=mesh['pipe'=8,'tensor'=4,'expert'=8] {'expert'}, dimensions={0} | all-to-all | bytes 655360 | tf_op jit(solution)/shard_map/while/body/eval_jaxpr/all_to_all | solution.py:92
  948.5 20.7 %all_to_all.93 = bf16[4,8,5,4096]{3,1,2,0:T(8,128)(2,1)S(1)} all-to-all(bf16[4,8,5,4096]{3,1,2,0:T(8,128)(2,1)S(1)} %broadcast_in_dim.48), channel_id=1, replica_groups=mesh['pipe'=8,'tensor'=4,'expert'=8] {'tensor'}, dimensions={0} | all-to-all | bytes 2621440 | tf_op jit(solution)/shard_map/while/body/eval_jaxpr/all_to_all | solution.py:11
  984.0 17.0 %all-to-all-done.3 = bf16[4,8,5,4096]{3,1,2,0:T(8,128)(2,1)S(1)} async-done(((bf16[4,8,5,4096]{3,1,2,0:T(8,128)(2,1)}), bf16[4,8,5,4096]{3,1,2,0:T(8,128)(2,1)S(1)}, u32[]{:S(2)}, u32[]{:S(2)}) %all-to-all-start.3) | async-done | bytes 1310752 | tf_op jit(solution)/shard_map/while/body/eval_jaxpr/all_to_all | solution.py:32
  1056.5 21.3 %all_to_all.92 = bf16[8,5,4096]{2,1,0:T(8,128)(2,1)S(1)} all-to-all(bf16[8,5,4096]{2,1,0:T(8,128)(2,1)S(1)} %reshape.340), channel_id=1, replica_groups=mesh['pipe'=8,'tensor'=4,'expert'=8] {'expert'}, dimensions={0} | all-to-all | bytes 655360 | tf_op jit(solution)/shard_map/while/body/eval_jaxpr/all_to_all | solution.py:92
  1078.2 20.7 %all_to_all.93 = bf16[4,8,5,4096]{3,1,2,0:T(8,128)(2,1)S(1)} all-to-all(bf16[4,8,5,4096]{3,1,2,0:T(8,128)(2,1)S(1)} %broadcast_in_dim.48), channel_id=1, replica_groups=mesh['pipe'=8,'tensor'=4,'expert'=8] {'tensor'}, dimensions={0} | all-to-all | bytes 2621440 | tf_op jit(solution)/shard_map/while/body/eval_jaxpr/all_to_all | solution.py:11
  (727 shorter events, 702.6 us)
Async XLA Ops:
  6.1 10.4 all-to-all-start
  73.3 20.6 %all-to-all-start.3 = ((bf16[4,8,5,4096]{3,1,2,0:T(8,128)(2,1)}), bf16[4,8,5,4096]{3,1,2,0:T(8,128)(2,1)S(1)}, u32[]{:S(2)}, u32[]{:S(2)}) async-start(bf16[4,8,5,4096]{3,1,2,0:T(8,128)(2,1)} %copy.62), calls=%async_computation.3 | async-start | bytes 2621440 | tf_op jit(solution)/shard_map/while/body/eval_jaxpr/all_to_all | solution.py:32
  95.2 21.5 %all-to-all-start.4 = ((bf16[8,5,4096]{2,1,0:T(8,128)(2,1)}), bf16[8,5,4096]{2,1,0:T(8,128)(2,1)S(1)}, u32[]{:S(2)}, u32[]{:S(2)}) async-start(bf16[8,5,4096]{2,1,0:T(8,128)(2,1)} %copy.63), calls=%async_computation.4 | async-start | bytes 1048576 | tf_op jit(solution)/shard_map/while/body/eval_jaxpr/all_to_all | solution.py:94
  119.3 9.3 all-to-all-start.5
  142.0 9.3 all-to-all-start
  203.4 20.7 %all-to-all-start.3 = ((bf16[4,8,5,4096]{3,1,2,0:T(8,128)(2,1)}), bf16[4,8,5,4096]{3,1,2,0:T(8,128)(2,1)S(1)}, u32[]{:S(2)}, u32[]{:S(2)}) async-start(bf16[4,8,5,4096]{3,1,2,0:T(8,128)(2,1)} %copy.62), calls=%async_computation.3 | async-start | bytes 2621440 | tf_op jit(solution)/shard_map/while/body/eval_jaxpr/all_to_all | solution.py:32
  225.4 18.7 %all-to-all-start.4 = ((bf16[8,5,4096]{2,1,0:T(8,128)(2,1)}), bf16[8,5,4096]{2,1,0:T(8,128)(2,1)S(1)}, u32[]{:S(2)}, u32[]{:S(2)}) async-start(bf16[8,5,4096]{2,1,0:T(8,128)(2,1)} %copy.63), calls=%async_computation.4 | async-start | bytes 1048576 | tf_op jit(solution)/shard_map/while/body/eval_jaxpr/all_to_all | solution.py:94
  246.8 9.3 all-to-all-start.5
  270.1 9.3 all-to-all-start
  331.7 20.7 %all-to-all-start.3 = ((bf16[4,8,5,4096]{3,1,2,0:T(8,128)(2,1)}), bf16[4,8,5,4096]{3,1,2,0:T(8,128)(2,1)S(1)}, u32[]{:S(2)}, u32[]{:S(2)}) async-start(bf16[4,8,5,4096]{3,1,2,0:T(8,128)(2,1)} %copy.62), calls=%async_computation.3 | async-start | bytes 2621440 | tf_op jit(solution)/shard_map/while/body/eval_jaxpr/all_to_all | solution.py:32
  353.7 18.6 %all-to-all-start.4 = ((bf16[8,5,4096]{2,1,0:T(8,128)(2,1)}), bf16[8,5,4096]{2,1,0:T(8,128)(2,1)S(1)}, u32[]{:S(2)}, u32[]{:S(2)}) async-start(bf16[8,5,4096]{2,1,0:T(8,128)(2,1)} %copy.63), calls=%async_computation.4 | async-start | bytes 1048576 | tf_op jit(solution)/shard_map/while/body/eval_jaxpr/all_to_all | solution.py:94
  375.0 9.3 all-to-all-start.5
  461.4 20.7 %all-to-all-start.3 = ((bf16[4,8,5,4096]{3,1,2,0:T(8,128)(2,1)}), bf16[4,8,5,4096]{3,1,2,0:T(8,128)(2,1)S(1)}, u32[]{:S(2)}, u32[]{:S(2)}) async-start(bf16[4,8,5,4096]{3,1,2,0:T(8,128)(2,1)} %copy.62), calls=%async_computation.3 | async-start | bytes 2621440 | tf_op jit(solution)/shard_map/while/body/eval_jaxpr/all_to_all | solution.py:32
  483.4 18.6 %all-to-all-start.4 = ((bf16[8,5,4096]{2,1,0:T(8,128)(2,1)}), bf16[8,5,4096]{2,1,0:T(8,128)(2,1)S(1)}, u32[]{:S(2)}, u32[]{:S(2)}) async-start(bf16[8,5,4096]{2,1,0:T(8,128)(2,1)} %copy.63), calls=%async_computation.4 | async-start | bytes 1048576 | tf_op jit(solution)/shard_map/while/body/eval_jaxpr/all_to_all | solution.py:94
  591.1 20.7 %all-to-all-start.3 = ((bf16[4,8,5,4096]{3,1,2,0:T(8,128)(2,1)}), bf16[4,8,5,4096]{3,1,2,0:T(8,128)(2,1)S(1)}, u32[]{:S(2)}, u32[]{:S(2)}) async-start(bf16[4,8,5,4096]{3,1,2,0:T(8,128)(2,1)} %copy.62), calls=%async_computation.3 | async-start | bytes 2621440 | tf_op jit(solution)/shard_map/while/body/eval_jaxpr/all_to_all | solution.py:32
  613.1 18.6 %all-to-all-start.4 = ((bf16[8,5,4096]{2,1,0:T(8,128)(2,1)}), bf16[8,5,4096]{2,1,0:T(8,128)(2,1)S(1)}, u32[]{:S(2)}, u32[]{:S(2)}) async-start(bf16[8,5,4096]{2,1,0:T(8,128)(2,1)} %copy.63), calls=%async_computation.4 | async-start | bytes 1048576 | tf_op jit(solution)/shard_map/while/body/eval_jaxpr/all_to_all | solution.py:94
  720.9 20.7 %all-to-all-start.3 = ((bf16[4,8,5,4096]{3,1,2,0:T(8,128)(2,1)}), bf16[4,8,5,4096]{3,1,2,0:T(8,128)(2,1)S(1)}, u32[]{:S(2)}, u32[]{:S(2)}) async-start(bf16[4,8,5,4096]{3,1,2,0:T(8,128)(2,1)} %copy.62), calls=%async_computation.3 | async-start | bytes 2621440 | tf_op jit(solution)/shard_map/while/body/eval_jaxpr/all_to_all | solution.py:32
  742.9 18.6 %all-to-all-start.4 = ((bf16[8,5,4096]{2,1,0:T(8,128)(2,1)}), bf16[8,5,4096]{2,1,0:T(8,128)(2,1)S(1)}, u32[]{:S(2)}, u32[]{:S(2)}) async-start(bf16[8,5,4096]{2,1,0:T(8,128)(2,1)} %copy.63), calls=%async_computation.4 | async-start | bytes 1048576 | tf_op jit(solution)/shard_map/while/body/eval_jaxpr/all_to_all | solution.py:94
  850.6 20.7 %all-to-all-start.3 = ((bf16[4,8,5,4096]{3,1,2,0:T(8,128)(2,1)}), bf16[4,8,5,4096]{3,1,2,0:T(8,128)(2,1)S(1)}, u32[]{:S(2)}, u32[]{:S(2)}) async-start(bf16[4,8,5,4096]{3,1,2,0:T(8,128)(2,1)} %copy.62), calls=%async_computation.3 | async-start | bytes 2621440 | tf_op jit(solution)/shard_map/while/body/eval_jaxpr/all_to_all | solution.py:32
  872.6 18.6 %all-to-all-start.4 = ((bf16[8,5,4096]{2,1,0:T(8,128)(2,1)}), bf16[8,5,4096]{2,1,0:T(8,128)(2,1)S(1)}, u32[]{:S(2)}, u32[]{:S(2)}) async-start(bf16[8,5,4096]{2,1,0:T(8,128)(2,1)} %copy.63), calls=%async_computation.4 | async-start | bytes 1048576 | tf_op jit(solution)/shard_map/while/body/eval_jaxpr/all_to_all | solution.py:94
  980.3 20.7 %all-to-all-start.3 = ((bf16[4,8,5,4096]{3,1,2,0:T(8,128)(2,1)}), bf16[4,8,5,4096]{3,1,2,0:T(8,128)(2,1)S(1)}, u32[]{:S(2)}, u32[]{:S(2)}) async-start(bf16[4,8,5,4096]{3,1,2,0:T(8,128)(2,1)} %copy.62), calls=%async_computation.3 | async-start | bytes 2621440 | tf_op jit(solution)/shard_map/while/body/eval_jaxpr/all_to_all | solution.py:32
  1002.3 18.6 %all-to-all-start.4 = ((bf16[8,5,4096]{2,1,0:T(8,128)(2,1)}), bf16[8,5,4096]{2,1,0:T(8,128)(2,1)S(1)}, u32[]{:S(2)}, u32[]{:S(2)}) async-start(bf16[8,5,4096]{2,1,0:T(8,128)(2,1)} %copy.63), calls=%async_computation.4 | async-start | bytes 1048576 | tf_op jit(solution)/shard_map/while/body/eval_jaxpr/all_to_all | solution.py:94
  1110.0 20.7 %all-to-all-start.3 = ((bf16[4,8,5,4096]{3,1,2,0:T(8,128)(2,1)}), bf16[4,8,5,4096]{3,1,2,0:T(8,128)(2,1)S(1)}, u32[]{:S(2)}, u32[]{:S(2)}) async-start(bf16[4,8,5,4096]{3,1,2,0:T(8,128)(2,1)} %copy.62), calls=%async_computation.3 | async-start | bytes 2621440 | tf_op jit(solution)/shard_map/while/body/eval_jaxpr/all_to_all | solution.py:32
  1132.0 18.6 %all-to-all-start.4 = ((bf16[8,5,4096]{2,1,0:T(8,128)(2,1)}), bf16[8,5,4096]{2,1,0:T(8,128)(2,1)S(1)}, u32[]{:S(2)}, u32[]{:S(2)}) async-start(bf16[8,5,4096]{2,1,0:T(8,128)(2,1)} %copy.63), calls=%async_computation.4 | async-start | bytes 1048576 | tf_op jit(solution)/shard_map/while/body/eval_jaxpr/all_to_all | solution.py:94
  (102 other events, 1011.6 us)
where the time goes:
time: 1180 us; the launch traced here: 1170 us
  waiting for transfers between devices  396 us (34%)
  blocking collectives  375 us (32%)
  starting transfers between devices  154 us (13%)
  local copies, waits for them, and re-layouts  115 us (10%)
  matrix products  67.2 us (6%)
  other arithmetic  56.2 us (5%)
    all_to_all x9, blocking collectives, expert_layer(): lax.all_to_all(outgoing, 'expert', split_axis=0, concat_axis=0, tiled=True)  189 us
    all_to_all x9, blocking collectives, from_everyone(): return lax.all_to_all(copies, axis, split_axis=0, concat_axis=0, tiled=True)  186 us
    all_to_all x9, waiting for transfers between devices, sum_at_owner(): lax.all_to_all(pieces, axis, split_axis=0, concat_axis=0, tiled=True)  153 us
    all_to_all x9, waiting for transfers between devices, expert_layer(): lax.all_to_all(returned, 'expert', split_axis=0, concat_axis=0, tiled=True)  130 us
    all_to_all x9, waiting for transfers between devices, run_section(): lax.all_to_all(fresh_rows, 'tensor', split_axis=1, concat_axis=0, tiled=T...  46.4 us
    dot_general x9, matrix products, expert_work(): jnp.dot(hidden, down_matrix, preferred_element_type=jnp.float32)  40.5 us
    ppermute x9, waiting for transfers between devices, passed_along(): return lax.ppermute(block, axis, route)  35 us
    all_to_all x9, starting transfers between devices, sum_at_owner(): lax.all_to_all(pieces, axis, split_axis=0, concat_axis=0, tiled=True)  33 us
  transfers between devices with their start and end apart: 45, of which 45 were waited for; matrix products, arithmetic and copies ran while one was open for 3% of the time, Pallas kernels for 0%

commit v1 on v0

--- a/solution.py
+++ b/solution.py
@@ -4,6 +4,17 @@
 from jax.sharding import PartitionSpec as P
 
 epsilon = 1e-06
+
+
+def cut_along_2(x, dim, size):
+    before, after = (x.shape[:dim], x.shape[dim + 1 :])
+    return jnp.moveaxis(x.reshape(*before, size, -1, *after), dim, 0)
+
+
+def in_order(blocks, dim):
+    blocks = jnp.moveaxis(blocks, 0, dim)
+    dims = blocks.shape
+    return blocks.reshape(*dims[:dim], dims[dim] * dims[dim + 1], *dims[dim + 2 :])
 
 
 def from_everyone(value, axis):
@@ -109,7 +120,14 @@
         order_all = picks[0, micro_index, 0]
         chosen = lax.dynamic_slice_in_dim(order_all, my_rank * quarter, quarter)
         permuted = stream[order_all]
-        quarter_rows = lax.all_to_all(permuted, "tensor", split_axis=0, concat_axis=1, tiled=True)
+        peers, index = (lax.axis_size("tensor"), lax.axis_index("tensor"))
+        tiles = cut_along_2(permuted, 0, peers)
+        outs = [tiles[index]]
+        for step in range(1, peers):
+            sent = tiles[index ^ step]
+            outs.append(lax.ppermute(sent, "tensor", [(i_2, i_2 ^ step) for i_2 in range(peers)]))
+        tiles = jnp.stack(outs)[index ^ jnp.arange(peers)]
+        quarter_rows = in_order(tiles, 1)
         fresh_rows = expert_layer(quarter_rows, chosen, micro_index)
         spread = lax.all_to_all(fresh_rows, "tensor", split_axis=1, concat_axis=0, tiled=True)
         return jnp.zeros_like(stream).at[order_all].set(spread)

time: 1180 us -> 1160 us (0.983)
  waiting for transfers between devices: 396 us -> 368 us
    ppermute x0 -> x27, starting transfers between devices: none -> 37.6 us  [run_section(): lax.ppermute(sent, 'tensor', [(i_2, i_2 ^ step) for i_2 in range(peers)])]
    all_to_all x9 -> x0, starting transfers between devices: 31 us -> none  [run_section(): lax.all_to_all(permuted, 'tensor', split_axis=0, concat_axis=1, tiled=True)]
    all_to_all x9 -> x0, waiting for transfers between devices: 31 us -> none  [run_section(): lax.all_to_all(permuted, 'tensor', split_axis=0, concat_axis=1, tiled=True)]
  transfers between devices with their start and end apart: 45 -> 63, of which waited for: 45 -> 37; matrix products, arithmetic and copies ran while one was open for 3% -> 3% of each run, Pallas kernels for 0% -> 0%
where the time goes in v1:
time: 1160 us; the launch traced here: 1150 us
  blocking collectives  378 us (33%)
  waiting for transfers between devices  368 us (32%)
  starting transfers between devices  156 us (13%)
  local copies, waits for them, and re-layouts  119 us (10%)
  matrix products  67.2 us (6%)
  other arithmetic  55.5 us (5%)
    all_to_all x9, blocking collectives, expert_layer(): lax.all_to_all(outgoing, 'expert', split_axis=0, concat_axis=0, tiled=True)  191 us
    all_to_all x9, blocking collectives, from_everyone(): return lax.all_to_all(copies, axis, split_axis=0, concat_axis=0, tiled=True)  186 us
    all_to_all x9, waiting for transfers between devices, sum_at_owner(): lax.all_to_all(pieces, axis, split_axis=0, concat_axis=0, tiled=True)  151 us
    all_to_all x9, waiting for transfers between devices, expert_layer(): lax.all_to_all(returned, 'expert', split_axis=0, concat_axis=0, tiled=True)  130 us
    all_to_all x9, waiting for transfers between devices, run_section(): lax.all_to_all(fresh_rows, 'tensor', split_axis=1, concat_axis=0, tiled=T...  46.8 us
    dot_general x9, matrix products, expert_work(): jnp.dot(hidden, down_matrix, preferred_element_type=jnp.float32)  40.5 us
    ppermute x9, waiting for transfers between devices, passed_along(): return lax.ppermute(block, axis, route)  37.8 us
    ppermute x27, starting transfers between devices, run_section(): lax.ppermute(sent, 'tensor', [(i_2, i_2 ^ step) for i_2 in range(peers)])  37.6 us
  transfers between devices with their start and end apart: 63, of which 37 were waited for; matrix products, arithmetic and copies ran while one was open for 3% of the time, Pallas kernels for 0%

profile of v1, /device:TPU:32, one launch (start us, length us, event | category | flops | bytes accessed | tf_op | source)
XLA Modules:
  0.0 1153.7 jit_solution(14323589501952192600)
XLA Ops:
  1.3 1152.4 %while.16 = (s32[]{:T(128)}, bf16[64,1024]{1,0:T(8,128)(2,1)S(1)}, bf16[2,64,1024]{2,1,0:T(8,128)(2,1)}, s32[9]{0:T(128)}, s32[]{:T(128)}, /*index=5*/s32[1,2,1,...) while((s32[]{:T(128)}, bf16[64,1024]{1,0:T(8,128)(2,1)S(1)}, ...), condition=%wide.region_8.9_spmd, body=%wide.region_0.8_spmd.sunk | while | flops 1523440896 | bytes 51867752 | solution.py:157
  15.8 23.8 %all_to_all.67 = bf16[8,5,4096]{2,1,0:T(8,128)(2,1)S(1)} all-to-all(bf16[8,5,4096]{2,1,0:T(8,128)(2,1)S(1)} %reshape.373), channel_id=1, replica_groups=mesh['pipe'=8,'tensor'=4,'expert'=8] {'expert'}, dimensions={0} | all-to-all | bytes 655360 | tf_op jit(solution)/shard_map/while/body/eval_jaxpr/all_to_all | solution.py:103
  39.9 20.8 %all_to_all.68 = bf16[4,8,5,4096]{3,1,2,0:T(8,128)(2,1)S(1)} all-to-all(bf16[4,8,5,4096]{3,1,2,0:T(8,128)(2,1)S(1)} %broadcast_in_dim.49), channel_id=1, replica_groups=mesh['pipe'=8,'tensor'=4,'expert'=8] {'tensor'}, dimensions={0} | all-to-all | bytes 2621440 | tf_op jit(solution)/shard_map/while/body/eval_jaxpr/all_to_all | solution.py:22
  98.1 16.9 %all-to-all-done.3 = bf16[8,5,4096]{2,1,0:T(8,128)(2,1)S(1)} async-done(((bf16[8,5,4096]{2,1,0:T(8,128)(2,1)}), bf16[8,5,4096]{2,1,0:T(8,128)(2,1)S(1)}, u32[]{:S(2)}, u32[]{:S(2)}) %all-to-all-start.3) | async-done | bytes 327712 | tf_op jit(solution)/shard_map/while/body/eval_jaxpr/all_to_all | solution.py:105
  148.7 18.9 %all_to_all.67 = bf16[8,5,4096]{2,1,0:T(8,128)(2,1)S(1)} all-to-all(bf16[8,5,4096]{2,1,0:T(8,128)(2,1)S(1)} %reshape.373), channel_id=1, replica_groups=mesh['pipe'=8,'tensor'=4,'expert'=8] {'expert'}, dimensions={0} | all-to-all | bytes 655360 | tf_op jit(solution)/shard_map/while/body/eval_jaxpr/all_to_all | solution.py:103
  168.0 20.7 %all_to_all.68 = bf16[4,8,5,4096]{3,1,2,0:T(8,128)(2,1)S(1)} all-to-all(bf16[4,8,5,4096]{3,1,2,0:T(8,128)(2,1)S(1)} %broadcast_in_dim.49), channel_id=1, replica_groups=mesh['pipe'=8,'tensor'=4,'expert'=8] {'tensor'}, dimensions={0} | all-to-all | bytes 2621440 | tf_op jit(solution)/shard_map/while/body/eval_jaxpr/all_to_all | solution.py:22
  274.6 20.6 %all_to_all.67 = bf16[8,5,4096]{2,1,0:T(8,128)(2,1)S(1)} all-to-all(bf16[8,5,4096]{2,1,0:T(8,128)(2,1)S(1)} %reshape.373), channel_id=1, replica_groups=mesh['pipe'=8,'tensor'=4,'expert'=8] {'expert'}, dimensions={0} | all-to-all | bytes 655360 | tf_op jit(solution)/shard_map/while/body/eval_jaxpr/all_to_all | solution.py:103
  295.5 20.7 %all_to_all.68 = bf16[4,8,5,4096]{3,1,2,0:T(8,128)(2,1)S(1)} all-to-all(bf16[4,8,5,4096]{3,1,2,0:T(8,128)(2,1)S(1)} %broadcast_in_dim.49), channel_id=1, replica_groups=mesh['pipe'=8,'tensor'=4,'expert'=8] {'tensor'}, dimensions={0} | all-to-all | bytes 2621440 | tf_op jit(solution)/shard_map/while/body/eval_jaxpr/all_to_all | solution.py:22
  331.1 16.8 %all-to-all-done.2 = bf16[4,8,5,4096]{3,1,2,0:T(8,128)(2,1)S(1)} async-done(((bf16[4,8,5,4096]{3,1,2,0:T(8,128)(2,1)}), bf16[4,8,5,4096]{3,1,2,0:T(8,128)(2,1)S(1)}, u32[]{:S(2)}, u32[]{:S(2)}) %all-to-all-start.2) | async-done | bytes 1310752 | tf_op jit(solution)/shard_map/while/body/eval_jaxpr/all_to_all | solution.py:43
  401.4 21.3 %all_to_all.67 = bf16[8,5,4096]{2,1,0:T(8,128)(2,1)S(1)} all-to-all(bf16[8,5,4096]{2,1,0:T(8,128)(2,1)S(1)} %reshape.373), channel_id=1, replica_groups=mesh['pipe'=8,'tensor'=4,'expert'=8] {'expert'}, dimensions={0} | all-to-all | bytes 655360 | tf_op jit(solution)/shard_map/while/body/eval_jaxpr/all_to_all | solution.py:103
  423.1 20.7 %all_to_all.68 = bf16[4,8,5,4096]{3,1,2,0:T(8,128)(2,1)S(1)} all-to-all(bf16[4,8,5,4096]{3,1,2,0:T(8,128)(2,1)S(1)} %broadcast_in_dim.49), channel_id=1, replica_groups=mesh['pipe'=8,'tensor'=4,'expert'=8] {'tensor'}, dimensions={0} | all-to-all | bytes 2621440 | tf_op jit(solution)/shard_map/while/body/eval_jaxpr/all_to_all | solution.py:22
  529.0 21.3 %all_to_all.67 = bf16[8,5,4096]{2,1,0:T(8,128)(2,1)S(1)} all-to-all(bf16[8,5,4096]{2,1,0:T(8,128)(2,1)S(1)} %reshape.373), channel_id=1, replica_groups=mesh['pipe'=8,'tensor'=4,'expert'=8] {'expert'}, dimensions={0} | all-to-all | bytes 655360 | tf_op jit(solution)/shard_map/while/body/eval_jaxpr/all_to_all | solution.py:103
  550.7 20.7 %all_to_all.68 = bf16[4,8,5,4096]{3,1,2,0:T(8,128)(2,1)S(1)} all-to-all(bf16[4,8,5,4096]{3,1,2,0:T(8,128)(2,1)S(1)} %broadcast_in_dim.49), channel_id=1, replica_groups=mesh['pipe'=8,'tensor'=4,'expert'=8] {'tensor'}, dimensions={0} | all-to-all | bytes 2621440 | tf_op jit(solution)/shard_map/while/body/eval_jaxpr/all_to_all | solution.py:22
  586.3 16.8 %all-to-all-done.2 = bf16[4,8,5,4096]{3,1,2,0:T(8,128)(2,1)S(1)} async-done(((bf16[4,8,5,4096]{3,1,2,0:T(8,128)(2,1)}), bf16[4,8,5,4096]{3,1,2,0:T(8,128)(2,1)S(1)}, u32[]{:S(2)}, u32[]{:S(2)}) %all-to-all-start.2) | async-done | bytes 1310752 | tf_op jit(solution)/shard_map/while/body/eval_jaxpr/all_to_all | solution.py:43
  656.6 21.3 %all_to_all.67 = bf16[8,5,4096]{2,1,0:T(8,128)(2,1)S(1)} all-to-all(bf16[8,5,4096]{2,1,0:T(8,128)(2,1)S(1)} %reshape.373), channel_id=1, replica_groups=mesh['pipe'=8,'tensor'=4,'expert'=8] {'expert'}, dimensions={0} | all-to-all | bytes 655360 | tf_op jit(solution)/shard_map/while/body/eval_jaxpr/all_to_all | solution.py:103
  678.3 20.7 %all_to_all.68 = bf16[4,8,5,4096]{3,1,2,0:T(8,128)(2,1)S(1)} all-to-all(bf16[4,8,5,4096]{3,1,2,0:T(8,128)(2,1)S(1)} %broadcast_in_dim.49), channel_id=1, replica_groups=mesh['pipe'=8,'tensor'=4,'expert'=8] {'tensor'}, dimensions={0} | all-to-all | bytes 2621440 | tf_op jit(solution)/shard_map/while/body/eval_jaxpr/all_to_all | solution.py:22
  784.1 21.3 %all_to_all.67 = bf16[8,5,4096]{2,1,0:T(8,128)(2,1)S(1)} all-to-all(bf16[8,5,4096]{2,1,0:T(8,128)(2,1)S(1)} %reshape.373), channel_id=1, replica_groups=mesh['pipe'=8,'tensor'=4,'expert'=8] {'expert'}, dimensions={0} | all-to-all | bytes 655360 | tf_op jit(solution)/shard_map/while/body/eval_jaxpr/all_to_all | solution.py:103
  805.8 20.7 %all_to_all.68 = bf16[4,8,5,4096]{3,1,2,0:T(8,128)(2,1)S(1)} all-to-all(bf16[4,8,5,4096]{3,1,2,0:T(8,128)(2,1)S(1)} %broadcast_in_dim.49), channel_id=1, replica_groups=mesh['pipe'=8,'tensor'=4,'expert'=8] {'tensor'}, dimensions={0} | all-to-all | bytes 2621440 | tf_op jit(solution)/shard_map/while/body/eval_jaxpr/all_to_all | solution.py:22
  841.4 16.8 %all-to-all-done.2 = bf16[4,8,5,4096]{3,1,2,0:T(8,128)(2,1)S(1)} async-done(((bf16[4,8,5,4096]{3,1,2,0:T(8,128)(2,1)}), bf16[4,8,5,4096]{3,1,2,0:T(8,128)(2,1)S(1)}, u32[]{:S(2)}, u32[]{:S(2)}) %all-to-all-start.2) | async-done | bytes 1310752 | tf_op jit(solution)/shard_map/while/body/eval_jaxpr/all_to_all | solution.py:43
  911.7 21.3 %all_to_all.67 = bf16[8,5,4096]{2,1,0:T(8,128)(2,1)S(1)} all-to-all(bf16[8,5,4096]{2,1,0:T(8,128)(2,1)S(1)} %reshape.373), channel_id=1, replica_groups=mesh['pipe'=8,'tensor'=4,'expert'=8] {'expert'}, dimensions={0} | all-to-all | bytes 655360 | tf_op jit(solution)/shard_map/while/body/eval_jaxpr/all_to_all | solution.py:103
  933.4 20.7 %all_to_all.68 = bf16[4,8,5,4096]{3,1,2,0:T(8,128)(2,1)S(1)} all-to-all(bf16[4,8,5,4096]{3,1,2,0:T(8,128)(2,1)S(1)} %broadcast_in_dim.49), channel_id=1, replica_groups=mesh['pipe'=8,'tensor'=4,'expert'=8] {'tensor'}, dimensions={0} | all-to-all | bytes 2621440 | tf_op jit(solution)/shard_map/while/body/eval_jaxpr/all_to_all | solution.py:22
  1039.3 21.3 %all_to_all.67 = bf16[8,5,4096]{2,1,0:T(8,128)(2,1)S(1)} all-to-all(bf16[8,5,4096]{2,1,0:T(8,128)(2,1)S(1)} %reshape.373), channel_id=1, replica_groups=mesh['pipe'=8,'tensor'=4,'expert'=8] {'expert'}, dimensions={0} | all-to-all | bytes 655360 | tf_op jit(solution)/shard_map/while/body/eval_jaxpr/all_to_all | solution.py:103
  1061.0 20.7 %all_to_all.68 = bf16[4,8,5,4096]{3,1,2,0:T(8,128)(2,1)S(1)} all-to-all(bf16[4,8,5,4096]{3,1,2,0:T(8,128)(2,1)S(1)} %broadcast_in_dim.49), channel_id=1, replica_groups=mesh['pipe'=8,'tensor'=4,'expert'=8] {'tensor'}, dimensions={0} | all-to-all | bytes 2621440 | tf_op jit(solution)/shard_map/while/body/eval_jaxpr/all_to_all | solution.py:22
  1096.5 16.8 %all-to-all-done.2 = bf16[4,8,5,4096]{3,1,2,0:T(8,128)(2,1)S(1)} async-done(((bf16[4,8,5,4096]{3,1,2,0:T(8,128)(2,1)}), bf16[4,8,5,4096]{3,1,2,0:T(8,128)(2,1)S(1)}, u32[]{:S(2)}, u32[]{:S(2)}) %all-to-all-start.2) | async-done | bytes 1310752 | tf_op jit(solution)/shard_map/while/body/eval_jaxpr/all_to_all | solution.py:43
  (808 shorter events, 682.3 us)
Async XLA Ops:
  71.9 20.5 %all-to-all-start.2 = ((bf16[4,8,5,4096]{3,1,2,0:T(8,128)(2,1)}), bf16[4,8,5,4096]{3,1,2,0:T(8,128)(2,1)S(1)}, u32[]{:S(2)}, u32[]{:S(2)}) async-start(bf16[4,8,5,4096]{3,1,2,0:T(8,128)(2,1)} %copy.57), calls=%async_computation.2 | async-start | bytes 2621440 | tf_op jit(solution)/shard_map/while/body/eval_jaxpr/all_to_all | solution.py:43
  93.7 21.4 %all-to-all-start.3 = ((bf16[8,5,4096]{2,1,0:T(8,128)(2,1)}), bf16[8,5,4096]{2,1,0:T(8,128)(2,1)S(1)}, u32[]{:S(2)}, u32[]{:S(2)}) async-start(bf16[8,5,4096]{2,1,0:T(8,128)(2,1)} %copy.58), calls=%async_computation.3 | async-start | bytes 1048576 | tf_op jit(solution)/shard_map/while/body/eval_jaxpr/all_to_all | solution.py:105
  117.7 9.3 all-to-all-start.4
  199.8 20.6 %all-to-all-start.2 = ((bf16[4,8,5,4096]{3,1,2,0:T(8,128)(2,1)}), bf16[4,8,5,4096]{3,1,2,0:T(8,128)(2,1)S(1)}, u32[]{:S(2)}, u32[]{:S(2)}) async-start(bf16[4,8,5,4096]{3,1,2,0:T(8,128)(2,1)} %copy.57), calls=%async_computation.2 | async-start | bytes 2621440 | tf_op jit(solution)/shard_map/while/body/eval_jaxpr/all_to_all | solution.py:43
  221.7 18.7 %all-to-all-start.3 = ((bf16[8,5,4096]{2,1,0:T(8,128)(2,1)}), bf16[8,5,4096]{2,1,0:T(8,128)(2,1)S(1)}, u32[]{:S(2)}, u32[]{:S(2)}) async-start(bf16[8,5,4096]{2,1,0:T(8,128)(2,1)} %copy.58), calls=%async_computation.3 | async-start | bytes 1048576 | tf_op jit(solution)/shard_map/while/body/eval_jaxpr/all_to_all | solution.py:105
  243.1 9.3 all-to-all-start.4
  327.4 20.6 %all-to-all-start.2 = ((bf16[4,8,5,4096]{3,1,2,0:T(8,128)(2,1)}), bf16[4,8,5,4096]{3,1,2,0:T(8,128)(2,1)S(1)}, u32[]{:S(2)}, u32[]{:S(2)}) async-start(bf16[4,8,5,4096]{3,1,2,0:T(8,128)(2,1)} %copy.57), calls=%async_computation.2 | async-start | bytes 2621440 | tf_op jit(solution)/shard_map/while/body/eval_jaxpr/all_to_all | solution.py:43
  349.2 18.6 %all-to-all-start.3 = ((bf16[8,5,4096]{2,1,0:T(8,128)(2,1)}), bf16[8,5,4096]{2,1,0:T(8,128)(2,1)S(1)}, u32[]{:S(2)}, u32[]{:S(2)}) async-start(bf16[8,5,4096]{2,1,0:T(8,128)(2,1)} %copy.58), calls=%async_computation.3 | async-start | bytes 1048576 | tf_op jit(solution)/shard_map/while/body/eval_jaxpr/all_to_all | solution.py:105
  370.5 9.3 all-to-all-start.4
  455.0 20.6 %all-to-all-start.2 = ((bf16[4,8,5,4096]{3,1,2,0:T(8,128)(2,1)}), bf16[4,8,5,4096]{3,1,2,0:T(8,128)(2,1)S(1)}, u32[]{:S(2)}, u32[]{:S(2)}) async-start(bf16[4,8,5,4096]{3,1,2,0:T(8,128)(2,1)} %copy.57), calls=%async_computation.2 | async-start | bytes 2621440 | tf_op jit(solution)/shard_map/while/body/eval_jaxpr/all_to_all | solution.py:43
  476.8 18.6 %all-to-all-start.3 = ((bf16[8,5,4096]{2,1,0:T(8,128)(2,1)}), bf16[8,5,4096]{2,1,0:T(8,128)(2,1)S(1)}, u32[]{:S(2)}, u32[]{:S(2)}) async-start(bf16[8,5,4096]{2,1,0:T(8,128)(2,1)} %copy.58), calls=%async_computation.3 | async-start | bytes 1048576 | tf_op jit(solution)/shard_map/while/body/eval_jaxpr/all_to_all | solution.py:105
  498.1 9.3 all-to-all-start.4
  582.5 20.6 %all-to-all-start.2 = ((bf16[4,8,5,4096]{3,1,2,0:T(8,128)(2,1)}), bf16[4,8,5,4096]{3,1,2,0:T(8,128)(2,1)S(1)}, u32[]{:S(2)}, u32[]{:S(2)}) async-start(bf16[4,8,5,4096]{3,1,2,0:T(8,128)(2,1)} %copy.57), calls=%async_computation.2 | async-start | bytes 2621440 | tf_op jit(solution)/shard_map/while/body/eval_jaxpr/all_to_all | solution.py:43
  604.4 18.6 %all-to-all-start.3 = ((bf16[8,5,4096]{2,1,0:T(8,128)(2,1)}), bf16[8,5,4096]{2,1,0:T(8,128)(2,1)S(1)}, u32[]{:S(2)}, u32[]{:S(2)}) async-start(bf16[8,5,4096]{2,1,0:T(8,128)(2,1)} %copy.58), calls=%async_computation.3 | async-start | bytes 1048576 | tf_op jit(solution)/shard_map/while/body/eval_jaxpr/all_to_all | solution.py:105
  625.6 9.3 all-to-all-start.4
  710.1 20.6 %all-to-all-start.2 = ((bf16[4,8,5,4096]{3,1,2,0:T(8,128)(2,1)}), bf16[4,8,5,4096]{3,1,2,0:T(8,128)(2,1)S(1)}, u32[]{:S(2)}, u32[]{:S(2)}) async-start(bf16[4,8,5,4096]{3,1,2,0:T(8,128)(2,1)} %copy.57), calls=%async_computation.2 | async-start | bytes 2621440 | tf_op jit(solution)/shard_map/while/body/eval_jaxpr/all_to_all | solution.py:43
  731.9 18.6 %all-to-all-start.3 = ((bf16[8,5,4096]{2,1,0:T(8,128)(2,1)}), bf16[8,5,4096]{2,1,0:T(8,128)(2,1)S(1)}, u32[]{:S(2)}, u32[]{:S(2)}) async-start(bf16[8,5,4096]{2,1,0:T(8,128)(2,1)} %copy.58), calls=%async_computation.3 | async-start | bytes 1048576 | tf_op jit(solution)/shard_map/while/body/eval_jaxpr/all_to_all | solution.py:105
  753.2 9.3 all-to-all-start.4
  837.7 20.6 %all-to-all-start.2 = ((bf16[4,8,5,4096]{3,1,2,0:T(8,128)(2,1)}), bf16[4,8,5,4096]{3,1,2,0:T(8,128)(2,1)S(1)}, u32[]{:S(2)}, u32[]{:S(2)}) async-start(bf16[4,8,5,4096]{3,1,2,0:T(8,128)(2,1)} %copy.57), calls=%async_computation.2 | async-start | bytes 2621440 | tf_op jit(solution)/shard_map/while/body/eval_jaxpr/all_to_all | solution.py:43
  859.5 18.6 %all-to-all-start.3 = ((bf16[8,5,4096]{2,1,0:T(8,128)(2,1)}), bf16[8,5,4096]{2,1,0:T(8,128)(2,1)S(1)}, u32[]{:S(2)}, u32[]{:S(2)}) async-start(bf16[8,5,4096]{2,1,0:T(8,128)(2,1)} %copy.58), calls=%async_computation.3 | async-start | bytes 1048576 | tf_op jit(solution)/shard_map/while/body/eval_jaxpr/all_to_all | solution.py:105
  965.3 20.6 %all-to-all-start.2 = ((bf16[4,8,5,4096]{3,1,2,0:T(8,128)(2,1)}), bf16[4,8,5,4096]{3,1,2,0:T(8,128)(2,1)S(1)}, u32[]{:S(2)}, u32[]{:S(2)}) async-start(bf16[4,8,5,4096]{3,1,2,0:T(8,128)(2,1)} %copy.57), calls=%async_computation.2 | async-start | bytes 2621440 | tf_op jit(solution)/shard_map/while/body/eval_jaxpr/all_to_all | solution.py:43
  987.1 18.6 %all-to-all-start.3 = ((bf16[8,5,4096]{2,1,0:T(8,128)(2,1)}), bf16[8,5,4096]{2,1,0:T(8,128)(2,1)S(1)}, u32[]{:S(2)}, u32[]{:S(2)}) async-start(bf16[8,5,4096]{2,1,0:T(8,128)(2,1)} %copy.58), calls=%async_computation.3 | async-start | bytes 1048576 | tf_op jit(solution)/shard_map/while/body/eval_jaxpr/all_to_all | solution.py:105
  1092.8 20.6 %all-to-all-start.2 = ((bf16[4,8,5,4096]{3,1,2,0:T(8,128)(2,1)}), bf16[4,8,5,4096]{3,1,2,0:T(8,128)(2,1)S(1)}, u32[]{:S(2)}, u32[]{:S(2)}) async-start(bf16[4,8,5,4096]{3,1,2,0:T(8,128)(2,1)} %copy.57), calls=%async_computation.2 | async-start | bytes 2621440 | tf_op jit(solution)/shard_map/while/body/eval_jaxpr/all_to_all | solution.py:43
  1114.7 18.6 %all-to-all-start.3 = ((bf16[8,5,4096]{2,1,0:T(8,128)(2,1)}), bf16[8,5,4096]{2,1,0:T(8,128)(2,1)S(1)}, u32[]{:S(2)}, u32[]{:S(2)}) async-start(bf16[8,5,4096]{2,1,0:T(8,128)(2,1)} %copy.58), calls=%async_computation.3 | async-start | bytes 1048576 | tf_op jit(solution)/shard_map/while/body/eval_jaxpr/all_to_all | solution.py:105
  (120 other events, 1028.7 us)
